TPU v7x, 32 devices: a whole 2x2x4 slice. The times are simulated.
32 devices in a mesh: dp: 8 (over y, x, core), group: 4 (over z).
Axes of the slice: x: 2, y: 2, z: 4, core: 2. Of those that a mesh axis runs over, the one named last changes fastest.
Arguments:
- images: bfloat16 [4096, 512], P(('dp', 'group')), may hold values from -1 to 1
- texts: bfloat16 [4096, 512], P(('dp', 'group')), may hold values from -1 to 1
- log_scale: float32 [], replicated, may hold values from 2 to 2.7
Outputs:
- grad_images: bfloat16 [4096, 512], P(('dp', 'group'))
- grad_texts: bfloat16 [4096, 512], P(('dp', 'group'))
- loss: float32 [], replicated
- grad_scale: float32 [], replicated
All inputs are finite; a program needn't handle non-finite values.
Results may differ from a plain program's by a relative error of at most 0.0013.
The roundings to bfloat16 on the way count: a program that leaves them out, or rounds other values in their place, can miss the bound.
Values may be sent and summed in bfloat16 or wider, within the bound.
A program may use at most 128 MiB of HBM per device.

v0:
```python
import jax
import jax.numpy as jnp
from jax import lax
from jax.sharding import PartitionSpec as P


def body(images, texts, log_scale):
    row_count = images.shape[0]
    device_count = lax.axis_size(("dp", "group"))
    pair_total = row_count * device_count
    within = lax.all_gather(texts, "group", axis=0, tiled=True)
    texts_whole = lax.all_gather(within, "dp", axis=0, tiled=True)
    images_whole = lax.all_gather(images, ("dp", "group"), axis=0, tiled=True)
    logit_scale = jnp.exp(log_scale)
    first_pair = lax.axis_index(("dp", "group")) * row_count
    contract_last = (((1,), (1,)), ((), ()))
    contract_first = (((0,), (0,)), ((), ()))
    row_logits = logit_scale * lax.dot_general(
        images, texts_whole, contract_last, preferred_element_type=jnp.float32
    )
    row_top = jnp.max(row_logits, axis=1)
    row_lse = row_top + jnp.log(jnp.sum(jnp.exp(row_logits - row_top[:, None]), axis=1))
    paired = jnp.diagonal(lax.dynamic_slice_in_dim(row_logits, first_pair, row_count, 1))
    part_top = jnp.max(row_logits, axis=0)
    part_sum = jnp.sum(jnp.exp(row_logits - part_top[None, :]), axis=0)
    got_top, got_sum = (
        lax.all_to_all(
            part_top.reshape(device_count, row_count),
            ("dp", "group"),
            split_axis=0,
            concat_axis=0,
            tiled=True,
        ),
        lax.all_to_all(
            part_sum.reshape(device_count, row_count),
            ("dp", "group"),
            split_axis=0,
            concat_axis=0,
            tiled=True,
        ),
    )
    col_top = jnp.max(got_top, axis=0)
    col_lse = col_top + jnp.log(jnp.sum(got_sum * jnp.exp(got_top - col_top[None, :]), axis=0))
    row_whole, col_whole = (
        lax.all_gather(row_lse, ("dp", "group"), axis=0, tiled=True),
        lax.all_gather(col_lse, ("dp", "group"), axis=0, tiled=True),
    )
    own_pairs = (
        jnp.arange(pair_total)[None, :] == (first_pair + jnp.arange(row_count))[:, None]
    ).astype(jnp.float32)
    row_grad = (
        0.5 * (jnp.exp(row_logits - row_lse[:, None]) + jnp.exp(row_logits - col_whole[None, :]))
        - own_pairs
    )
    scale_part = jnp.sum(row_grad * row_logits)
    row_weights = row_grad.astype(jnp.bfloat16)
    grad_images = (
        logit_scale * jnp.dot(row_weights, texts_whole, preferred_element_type=jnp.float32)
    ).astype(jnp.bfloat16)
    col_logits = logit_scale * lax.dot_general(
        images_whole, texts, contract_last, preferred_element_type=jnp.float32
    )
    col_grad = (
        0.5 * (jnp.exp(col_logits - row_whole[:, None]) + jnp.exp(col_logits - col_lse[None, :]))
        - own_pairs.T
    )
    text_sum = logit_scale * lax.dot_general(
        col_grad.astype(jnp.bfloat16),
        images_whole,
        contract_first,
        preferred_element_type=jnp.float32,
    )
    grad_texts = text_sum.astype(jnp.bfloat16)
    loss_part = jnp.sum(row_lse) + jnp.sum(col_lse) - 2.0 * jnp.sum(paired)
    loss_total, scale_total = lax.psum((loss_part, scale_part), ("dp", "group"))
    return (grad_images, grad_texts, loss_total / (2.0 * pair_total), scale_total / pair_total)


def solution(mesh):
    in_specs = (P(("dp", "group"), None), P(("dp", "group"), None), P())
    out_specs = (P(("dp", "group"), None), P(("dp", "group"), None), P(), P())
    return jax.shard_map(body, mesh=mesh, in_specs=in_specs, out_specs=out_specs, check_vma=False)
```

profile of v0, /device:TPU:0, one launch (start us, length us, event | category | flops | bytes accessed | tf_op | source)
XLA Modules:
  0.0 281.2 jit_solution(1704532022172781684)
XLA Ops:
  7.2 0.0 all-gather.5.cloned.1.call-start
  7.2 19.3 %all_gather.15 = bf16[512,512]{1,0:T(8,128)(2,1)} all-gather(bf16[128,512]{1,0:T(8,128)(2,1)} %param.4), channel_id=1, replica_groups=mesh['dp'=8,'group'=4] {'group'}, dimensions={0}, use_global_device_ids=true | all-gather | bytes 655360 | tf_op jit(solution)/shard_map/all_gather | solution.py:11
  26.5 0.0 all-gather.5.cloned.1.call-update
  26.6 0.0 all-gather.7.cloned.1.call-start
  26.6 0.7 all-gather.7.cloned.1.call-update
  28.0 35.0 %all-gather.5.cloned.1.call-done = bf16[4096,512]{1,0:T(8,128)(2,1)} async-done(((bf16[512,512]{1,0:T(8,128)(2,1)}), bf16[4096,512]{1,0:T(8,128)(2,1)}) %all-gather.5.cloned.1.call-update) | async-done | bytes 4194320 | tf_op jit(solution)/shard_map/all_gather | solution.py:12
  63.1 4.4 %fusion.10 = (f32[128]{0:T(128)S(1)}, f32[4096]{0:T(1024)}, f32[128,4096]{1,0:T(8,128)S(1)}) fusion(bf16[128,512]{1,0:T(8,128)(2,1)} %param.3, bf16[4096,512]{1,0:T(8,128)(2,1)} %all-gather.5.cloned.1.call-done, f32[]{:T(128)S(6)} %exp.24), kind=kOutput, calls=%fused_computation.27 | convolution fusion | flops 538439552 | bytes 6439428 | tf_op jit(solution)/shard_map/dot_general | solution.py:18
  67.5 4.6 %all-to-all-start = ((f32[32,1,128]{2,1,0:T(1,128)}), f32[32,1,128]{2,1,0:T(1,128)S(1)}, u32[]{:S(2)}, u32[]{:S(2)}) async-start(f32[32,1,128]{2,1,0:T(1,128)} %bitcast), calls=%async_computation | async-start | bytes 32768 | tf_op jit(solution)/shard_map/all_to_all | solution.py:27
  72.1 2.0 exponential_reduce_fusion.1
  74.2 0.6 fusion.12
  74.8 4.5 %all-to-all-done = f32[32,1,128]{2,1,0:T(1,128)S(1)} async-done(((f32[32,1,128]{2,1,0:T(1,128)}), f32[32,1,128]{2,1,0:T(1,128)S(1)}, u32[]{:S(2)}, u32[]{:S(2)}) %all-to-all-start) | async-done | bytes 16416 | tf_op jit(solution)/shard_map/all_to_all | solution.py:27
  79.2 2.5 all-to-all-start.1
  81.8 1.2 gather_fusion
  83.1 0.6 reduce_sum.68
  84.3 0.1 reduce_max.29
  84.4 4.6 %all-to-all-done.1 = f32[32,1,128]{2,1,0:T(1,128)S(1)} async-done(((f32[32,1,128]{2,1,0:T(1,128)}), f32[32,1,128]{2,1,0:T(1,128)S(1)}, u32[]{:S(2)}, u32[]{:S(2)}) %all-to-all-start.1) | async-done | bytes 16416 | tf_op jit(solution)/shard_map/all_to_all | solution.py:34
  89.0 0.6 fusion.11
  90.9 64.1 %all-gather = f32[32,1,128]{2,1,0:T(1,128)S(1)} all-gather(f32[1,1,128]{2,1,0:T(1,128)S(1)} %bitcast.22), channel_id=1, replica_groups=mesh['dp'=8,'group'=4] {'dp','group'}, dimensions={0}, use_global_device_ids=true | all-gather | bytes 16896 | tf_op jit(solution)/shard_map/all_gather | solution.py:46
  155.0 1.5 multiply_reduce_fusion
  156.5 65.1 %all-gather.1 = f32[32,1,128]{2,1,0:T(1,128)S(1)} all-gather(f32[1,1,128]{2,1,0:T(1,128)S(1)} %bitcast.21), channel_id=1, replica_groups=mesh['dp'=8,'group'=4] {'dp','group'}, dimensions={0}, use_global_device_ids=true | all-gather | bytes 16896 | tf_op jit(solution)/shard_map/all_gather | solution.py:45
  221.6 38.4 %all-reduce = (f32[]{:T(128)}, f32[]{:T(128)}) all-reduce(f32[]{:T(128)S(6)} %sub.81, f32[]{:T(128)} %multiply_reduce_fusion), channel_id=1, replica_groups=mesh['dp'=8,'group'=4] {'dp','group'}, use_global_device_ids=true, to_apply=%region_9.10 | all-reduce | flops 2 | bytes 16 | tf_op jit(solution)/shard_map/psum | solution.py:75
  261.4 0.0 copy-start
  261.4 4.0 %fusion.1 = bf16[128,512]{1,0:T(8,128)(2,1)} fusion(bf16[4096,512]{1,0:T(8,128)(2,1)} %all-gather.5.cloned.1.call-done, f32[128,4096]{1,0:T(8,128)S(1)} %get-tuple-element.14, s32[128]{0:T(128)S(1)} %iota_add_fusion, f32[4096]{0:T(1024)S(1)} %bitcast.18, f32[128]{0:T(128)S(1)} %get-tuple-element.13, f32[]{:T(128)S(6)} %exp.24), kind=kOutput, calls=%fused_computation.13 | convolution fusion | flops 541196288 | bytes 6439940 | tf_op jit(solution)/shard_map/dot_general | solution.py:58
  265.4 0.0 all-gather.7.cloned.1.call-done
  265.4 0.0 copy-done
  265.4 6.7 %fusion.2 = bf16[128,512]{1,0:T(8,128)(2,1)} fusion(bf16[4096,512]{1,0:T(8,128)(2,1)} %all-gather.7.cloned.1.call-done, bf16[128,512]{1,0:T(8,128)(2,1)S(1)} %copy-done, s32[128]{0:T(128)S(1)} %iota_add_fusion, f32[128]{0:T(128)S(1)} %get-tuple-element.11, f32[4096]{0:T(1024)S(1)} %bitcast.20, f32[]{:T(128)S(6)} %exp.24), kind=kOutput, calls=%fused_computation.14 | convolution fusion | flops 1078591488 | bytes 4473860 | tf_op jit(solution)/shard_map/dot_general | solution.py:67
  (4 shorter events, 0.1 us)
Async XLA Ops:
  7.2 55.9 %all-gather.5.cloned.1.call-start = ((), (), s32[]{:S(2)}) async-start(), calls=%async_computation.2 | async-start | bytes 4718592 | tf_op jit(solution)/shard_map/all_gather | solution.py:12
  26.6 238.8 %all-gather.7.cloned.1.call-start = ((), (), s32[]{:S(2)}) async-start(), calls=%async_computation.3 | async-start | bytes 4325376 | tf_op jit(solution)/shard_map/all_gather | solution.py:13
  67.5 11.7 %all-to-all-start = ((f32[32,1,128]{2,1,0:T(1,128)}), f32[32,1,128]{2,1,0:T(1,128)S(1)}, u32[]{:S(2)}, u32[]{:S(2)}) async-start(f32[32,1,128]{2,1,0:T(1,128)} %bitcast), calls=%async_computation | async-start | bytes 32768 | tf_op jit(solution)/shard_map/all_to_all | solution.py:27
  79.2 9.7 %all-to-all-start.1 = ((f32[32,1,128]{2,1,0:T(1,128)}), f32[32,1,128]{2,1,0:T(1,128)S(1)}, u32[]{:S(2)}, u32[]{:S(2)}) async-start(f32[32,1,128]{2,1,0:T(1,128)} %bitcast.1), calls=%async_computation.1 | async-start | bytes 32768 | tf_op jit(solution)/shard_map/all_to_all | solution.py:34
  261.4 4.0 %copy-start = (bf16[128,512]{1,0:T(8,128)(2,1)S(1)}, bf16[128,512]{1,0:T(8,128)(2,1)}, u32[]{:S(2)}) copy-start(bf16[128,512]{1,0:T(8,128)(2,1)} %param.4) | copy-start | bytes 393220
Sparse Core Ops, SparseCore 0:
  26.7 36.3 all-gather.4
  66.1 61.6 all-gather.6
where the time goes:
time: 282 us; the launch traced here: 281 us
  blocking collectives  187 us (66%)
  waiting for transfers between devices  44.8 us (16%)
  between operations  20.3 us (7%)
  matrix products  15.1 us (5%)
  starting transfers between devices  7.21 us (3%)
  other arithmetic  5.48 us (2%)
    all_gather x1, blocking collectives, body(): lax.all_gather(row_lse, ('dp', 'group'), axis=0, tiled=True)  65.1 us
    all_gather x1, blocking collectives, body(): lax.all_gather(col_lse, ('dp', 'group'), axis=0, tiled=True)  64.1 us
    psum x1, blocking collectives, body(): loss_total, scale_total = lax.psum((loss_part, scale_part), ('dp', 'group'))  38.4 us
    all_gather x1, waiting for transfers between devices, body(): texts_whole = lax.all_gather(within, 'dp', axis=0, tiled=True)  35 us
    all_gather x1, blocking collectives, body(): within = lax.all_gather(texts, 'group', axis=0, tiled=True)  19.3 us
    dot_general x1, matrix products, body(): lax.dot_general(col_grad.astype(jnp.bfloat16), images_whole, contract_fir...  6.7 us
  transfers between devices with their start and end apart: 4, of which 3 were waited for; matrix products, arithmetic and copies ran while one was open for 5% of the time, Pallas kernels for 0%

commit v1 on v0

--- a/solution.py
+++ b/solution.py
@@ -72,7 +72,7 @@
     )
     grad_texts = text_sum.astype(jnp.bfloat16)
     loss_part = jnp.sum(row_lse) + jnp.sum(col_lse) - 2.0 * jnp.sum(paired)
-    loss_total, scale_total = lax.psum((loss_part, scale_part), ("dp", "group"))
+    loss_total, scale_total = lax.psum(lax.psum((loss_part, scale_part), "group"), "dp")
     return (grad_images, grad_texts, loss_total / (2.0 * pair_total), scale_total / pair_total)
 
 

time: 282 us -> 265 us (0.940)
  blocking collectives: 187 us -> 170 us
    psum x1 -> x2, blocking collectives: 38.4 us -> 22 us  [the longest x1 12.4 us: body(): lax.psum(lax.psum((loss_part, scale_part), 'group'), 'dp')]
  transfers between devices with their start and end apart: 4 -> 4, of which waited for: 3 -> 3; matrix products, arithmetic and copies ran while one was open for 5% -> 6% of each run, Pallas kernels for 0% -> 0%
where the time goes in v1:
time: 265 us
  blocking collectives  170 us (64%)
  waiting for transfers between devices  44.8 us (17%)
  between operations  20.3 us (8%)
  matrix products  15.1 us (6%)
  starting transfers between devices  7.21 us (3%)
  other arithmetic  5.48 us (2%)
    all_gather x1, blocking collectives, body(): lax.all_gather(row_lse, ('dp', 'group'), axis=0, tiled=True)  65.1 us
    all_gather x1, blocking collectives, body(): lax.all_gather(col_lse, ('dp', 'group'), axis=0, tiled=True)  64.1 us
    all_gather x1, waiting for transfers between devices, body(): texts_whole = lax.all_gather(within, 'dp', axis=0, tiled=True)  35 us
    all_gather x1, blocking collectives, body(): within = lax.all_gather(texts, 'group', axis=0, tiled=True)  19.3 us
    psum x1, blocking collectives, body(): lax.psum(lax.psum((loss_part, scale_part), 'group'), 'dp')  12.4 us
    psum x1, blocking collectives, body(): lax.psum((loss_part, scale_part), 'group')  9.57 us
    dot_general x1, matrix products, body(): lax.dot_general(col_grad.astype(jnp.bfloat16), images_whole, contract_fir...  6.7 us
  transfers between devices with their start and end apart: 4, of which 3 were waited for; matrix products, arithmetic and copies ran while one was open for 6% of the time, Pallas kernels for 0%

profile of v1, /device:TPU:0, one launch (start us, length us, event | category | flops | bytes accessed | tf_op | source)
XLA Modules:
  0.0 264.7 jit_solution(10815658415297479351)
XLA Ops:
  7.2 0.0 all-gather.5.cloned.1.call-start
  7.2 19.3 %all_gather.15 = bf16[512,512]{1,0:T(8,128)(2,1)} all-gather(bf16[128,512]{1,0:T(8,128)(2,1)} %param.4), channel_id=1, replica_groups=mesh['dp'=8,'group'=4] {'group'}, dimensions={0}, use_global_device_ids=true | all-gather | bytes 655360 | tf_op jit(solution)/shard_map/all_gather | solution.py:11
  26.5 0.0 all-gather.5.cloned.1.call-update
  26.6 0.0 all-gather.7.cloned.1.call-start
  26.6 0.7 all-gather.7.cloned.1.call-update
  28.0 35.0 %all-gather.5.cloned.1.call-done = bf16[4096,512]{1,0:T(8,128)(2,1)} async-done(((bf16[512,512]{1,0:T(8,128)(2,1)}), bf16[4096,512]{1,0:T(8,128)(2,1)}) %all-gather.5.cloned.1.call-update) | async-done | bytes 4194320 | tf_op jit(solution)/shard_map/all_gather | solution.py:12
  63.1 4.4 %fusion.10 = (f32[128]{0:T(128)S(1)}, f32[4096]{0:T(1024)}, f32[128,4096]{1,0:T(8,128)S(1)}) fusion(bf16[128,512]{1,0:T(8,128)(2,1)} %param.3, bf16[4096,512]{1,0:T(8,128)(2,1)} %all-gather.5.cloned.1.call-done, f32[]{:T(128)S(6)} %exp.24), kind=kOutput, calls=%fused_computation.27 | convolution fusion | flops 538439552 | bytes 6439428 | tf_op jit(solution)/shard_map/dot_general | solution.py:18
  67.5 4.6 %all-to-all-start = ((f32[32,1,128]{2,1,0:T(1,128)}), f32[32,1,128]{2,1,0:T(1,128)S(1)}, u32[]{:S(2)}, u32[]{:S(2)}) async-start(f32[32,1,128]{2,1,0:T(1,128)} %bitcast), calls=%async_computation | async-start | bytes 32768 | tf_op jit(solution)/shard_map/all_to_all | solution.py:27
  72.1 2.0 exponential_reduce_fusion.1
  74.2 0.6 fusion.12
  74.8 4.5 %all-to-all-done = f32[32,1,128]{2,1,0:T(1,128)S(1)} async-done(((f32[32,1,128]{2,1,0:T(1,128)}), f32[32,1,128]{2,1,0:T(1,128)S(1)}, u32[]{:S(2)}, u32[]{:S(2)}) %all-to-all-start) | async-done | bytes 16416 | tf_op jit(solution)/shard_map/all_to_all | solution.py:27
  79.2 2.5 all-to-all-start.1
  81.8 1.2 gather_fusion
  83.1 0.6 reduce_sum.68
  84.3 0.1 reduce_max.29
  84.4 4.6 %all-to-all-done.1 = f32[32,1,128]{2,1,0:T(1,128)S(1)} async-done(((f32[32,1,128]{2,1,0:T(1,128)}), f32[32,1,128]{2,1,0:T(1,128)S(1)}, u32[]{:S(2)}, u32[]{:S(2)}) %all-to-all-start.1) | async-done | bytes 16416 | tf_op jit(solution)/shard_map/all_to_all | solution.py:34
  89.0 0.6 fusion.11
  90.9 64.1 %all-gather = f32[32,1,128]{2,1,0:T(1,128)S(1)} all-gather(f32[1,1,128]{2,1,0:T(1,128)S(1)} %bitcast.22), channel_id=1, replica_groups=mesh['dp'=8,'group'=4] {'dp','group'}, dimensions={0}, use_global_device_ids=true | all-gather | bytes 16896 | tf_op jit(solution)/shard_map/all_gather | solution.py:46
  155.0 1.5 multiply_reduce_fusion
  156.5 65.1 %all-gather.1 = f32[32,1,128]{2,1,0:T(1,128)S(1)} all-gather(f32[1,1,128]{2,1,0:T(1,128)S(1)} %bitcast.21), channel_id=1, replica_groups=mesh['dp'=8,'group'=4] {'dp','group'}, dimensions={0}, use_global_device_ids=true | all-gather | bytes 16896 | tf_op jit(solution)/shard_map/all_gather | solution.py:45
  221.6 9.6 %all-reduce.1 = (f32[]{:T(128)}, f32[]{:T(128)}) all-reduce(f32[]{:T(128)S(6)} %sub.81, f32[]{:T(128)} %multiply_reduce_fusion), channel_id=1, replica_groups=mesh['dp'=8,'group'=4] {'group'}, use_global_device_ids=true, to_apply=%region_9.10 | all-reduce | flops 2 | bytes 16 | tf_op jit(solution)/shard_map/psum | solution.py:75
  231.2 12.4 %all-reduce = (f32[]{:T(128)}, f32[]{:T(128)}) all-reduce(f32[]{:T(128)} %get-tuple-element.10, f32[]{:T(128)} %get-tuple-element.11), channel_id=1, replica_groups=mesh['dp'=8,'group'=4] {'dp'}, use_global_device_ids=true, to_apply=%region_10.11 | all-reduce | flops 2 | bytes 16 | tf_op jit(solution)/shard_map/psum | solution.py:75
  244.9 0.0 copy-start
  244.9 4.0 %fusion.1 = bf16[128,512]{1,0:T(8,128)(2,1)} fusion(bf16[4096,512]{1,0:T(8,128)(2,1)} %all-gather.5.cloned.1.call-done, f32[128,4096]{1,0:T(8,128)S(1)} %get-tuple-element.16, s32[128]{0:T(128)S(1)} %iota_add_fusion, f32[4096]{0:T(1024)S(1)} %bitcast.18, f32[128]{0:T(128)S(1)} %get-tuple-element.15, f32[]{:T(128)S(6)} %exp.24), kind=kOutput, calls=%fused_computation.13 | convolution fusion | flops 541196288 | bytes 6439940 | tf_op jit(solution)/shard_map/dot_general | solution.py:58
  248.9 0.0 all-gather.7.cloned.1.call-done
  248.9 0.0 copy-done
  248.9 6.7 %fusion.2 = bf16[128,512]{1,0:T(8,128)(2,1)} fusion(bf16[4096,512]{1,0:T(8,128)(2,1)} %all-gather.7.cloned.1.call-done, bf16[128,512]{1,0:T(8,128)(2,1)S(1)} %copy-done, s32[128]{0:T(128)S(1)} %iota_add_fusion, f32[128]{0:T(128)S(1)} %get-tuple-element.13, f32[4096]{0:T(1024)S(1)} %bitcast.20, f32[]{:T(128)S(6)} %exp.24), kind=kOutput, calls=%fused_computation.14 | convolution fusion | flops 1078591488 | bytes 4473860 | tf_op jit(solution)/shard_map/dot_general | solution.py:67
  (4 shorter events, 0.1 us)
Async XLA Ops:
  7.2 55.9 %all-gather.5.cloned.1.call-start = ((), (), s32[]{:S(2)}) async-start(), calls=%async_computation.2 | async-start | bytes 4718592 | tf_op jit(solution)/shard_map/all_gather | solution.py:12
  26.6 222.3 %all-gather.7.cloned.1.call-start = ((), (), s32[]{:S(2)}) async-start(), calls=%async_computation.3 | async-start | bytes 4325376 | tf_op jit(solution)/shard_map/all_gather | solution.py:13
  67.5 11.7 %all-to-all-start = ((f32[32,1,128]{2,1,0:T(1,128)}), f32[32,1,128]{2,1,0:T(1,128)S(1)}, u32[]{:S(2)}, u32[]{:S(2)}) async-start(f32[32,1,128]{2,1,0:T(1,128)} %bitcast), calls=%async_computation | async-start | bytes 32768 | tf_op jit(solution)/shard_map/all_to_all | solution.py:27
  79.2 9.7 %all-to-all-start.1 = ((f32[32,1,128]{2,1,0:T(1,128)}), f32[32,1,128]{2,1,0:T(1,128)S(1)}, u32[]{:S(2)}, u32[]{:S(2)}) async-start(f32[32,1,128]{2,1,0:T(1,128)} %bitcast.1), calls=%async_computation.1 | async-start | bytes 32768 | tf_op jit(solution)/shard_map/all_to_all | solution.py:34
  244.9 4.0 %copy-start = (bf16[128,512]{1,0:T(8,128)(2,1)S(1)}, bf16[128,512]{1,0:T(8,128)(2,1)}, u32[]{:S(2)}) copy-start(bf16[128,512]{1,0:T(8,128)(2,1)} %param.4) | copy-start | bytes 393220
Sparse Core Ops, SparseCore 0:
  26.7 36.3 all-gather.4
  66.1 61.6 all-gather.6
